TPU v7x, 32 devices: a whole 2x2x4 slice. The times are simulated.
32 devices in a mesh: dp: 8 (over z, x), section: 4 (over y, core).
Axes of the slice: x: 2, y: 2, z: 4, core: 2. Of those that a mesh axis runs over, the one named last changes fastest.
Arguments:
- activations: bfloat16 [4, 16, 512, 4096], P('section', 'dp'), may hold values from -16 to 16
- out_grads: bfloat16 [4, 16, 512, 1024], P('section', 'dp'), may hold values from -16 to 16
- lengths: int32 [16], P('dp'), may hold values from 64 to 512, as said below
Outputs:
- mean_grad: bfloat16 [4, 4096, 1024], P('section', 'dp')
- norm_ratio: float32 [16], P('dp')
Inputs may be any that keep to these rules, and one draw needn't show every extreme that they name: Example e's first lengths[e] token slots are real, the rest padding; some example fills all 512 slots.
All inputs are finite; a program needn't handle non-finite values.
Results may differ from a plain program's by a relative error of at most 0.015.
Values may be sent and summed in bfloat16 or wider, within the bound.
A program may use at most 128 MiB of HBM per device.

v0:
```python
import math

import jax
import jax.numpy as jnp
from jax import lax
from jax.sharding import PartitionSpec as P


def entering(value, axis, combine, identity):
    peers, mine = (lax.axis_size(axis), lax.axis_index(axis))
    everything = lax.all_gather(value, axis)
    start = jnp.broadcast_to(jnp.asarray(identity, value.dtype), value.shape)

    def lap(k, before):
        at = peers - 1 - k
        reached = at > mine
        new = combine(before, everything[at])
        return jnp.where(reached, new, before)

    return lax.fori_loop(0, peers, lap, start)


def from_root(value, axis, source):
    kept = jnp.where(lax.axis_index(axis) == source, value, 0).astype(value.dtype)
    return lax.psum(kept, axis)


def add_norms(earlier, later):
    return earlier + later


def row_term(flat_acts, flat_scaled, layer_index):
    columns = flat_acts[layer_index]
    return lax.dot_general(
        columns,
        flat_scaled[layer_index],
        (((0,), (0,)), ((), ())),
        preferred_element_type=jnp.float32,
    )


def on_device(activations, out_grads, lengths):
    layer_count, example_count, seq_len, model_width = activations.shape
    key_width = out_grads.shape[3]
    total_layers = layer_count * lax.axis_size("section")
    clip_bound = 0.5 * math.sqrt(float(total_layers * seq_len * model_width * key_width))
    positions = lax.broadcasted_iota(jnp.int32, (example_count, seq_len), 1)
    token_keep = (positions < lengths[:, None]).astype(jnp.bfloat16)
    masked = out_grads * token_keep[None, :, :, None]
    act_gram = jnp.einsum(
        "lesd,letd->lest", activations, activations, preferred_element_type=jnp.float32
    )
    grad_gram = jnp.einsum("lesk,letk->lest", masked, masked, preferred_element_type=jnp.float32)
    own_norms = jnp.sum(act_gram * grad_gram, axis=(0, 2, 3))
    later_norms = entering(own_norms, "section", add_norms, jnp.zeros_like(own_norms))
    norm_total = from_root(later_norms + own_norms, "section", 0)
    norm_ratio = jnp.sqrt(norm_total) / clip_bound
    clip_factor = 1.0 / jnp.maximum(norm_ratio, 1.0)
    scaled = (clip_factor[None, :, None, None] * masked).astype(jnp.bfloat16)
    flat_acts = activations.reshape(layer_count, example_count * seq_len, model_width)
    flat_scaled = scaled.reshape(layer_count, example_count * seq_len, key_width)
    examples_all = lax.axis_size("dp") * example_count
    pieces = [
        lax.psum_scatter(
            row_term(flat_acts, flat_scaled, 0).astype(jnp.bfloat16),
            "dp",
            scatter_dimension=0,
            tiled=True,
        ).astype(jnp.float32)
    ]
    stacked = jnp.stack(pieces)
    mean_grad = (stacked / examples_all).astype(jnp.bfloat16)
    return (mean_grad, norm_ratio)


def solution(mesh):
    placed = (P("section", "dp", None, None), P("section", "dp", None, None), P("dp"))
    return jax.shard_map(
        on_device,
        mesh=mesh,
        in_specs=placed,
        out_specs=(P("section", "dp", None), P("dp")),
        check_vma=False,
    )
```

profile of v0, /device:TPU:0, one launch (start us, length us, event | category | flops | bytes accessed | tf_op | source)
XLA Modules:
  0.0 212.2 jit_solution(11250981878342010992)
XLA Ops:
  7.2 0.0 reduce-scatter.2.cloned.1.call-start
  7.2 0.7 compare_convert_fusion
  8.0 1.3 dynamic-slice
  10.0 3.6 %fusion.8 = f32[2,512,512]{2,1,0:T(8,128)S(1)} fusion(bf16[1,2,512,1024]{3,2,1,0:T(8,128)(2,1)} %param.6, bf16[2,512]{1,0:T(2,128)(2,1)S(1)} %compare_convert_fusion), kind=kOutput, calls=%fused_computation.9 | convolution fusion | flops 1074790400 | bytes 4196352 | tf_op jit(solution)/shard_map/lesk,letk->lest/dot_general | solution.py:53
  13.6 0.0 copy-start
  13.6 10.7 %multiply_reduce_fusion = f32[2]{0:T(128)S(1)} fusion(f32[2,512,512]{2,1,0:T(8,128)S(1)} %fusion.8, bf16[1,2,512,4096]{3,2,1,0:T(8,128)(2,1)} %param.5), kind=kOutput, calls=%fused_computation.13 | convolution fusion | flops 4296015872 | bytes 10485768 | tf_op jit(solution)/shard_map/lesd,letd->lest/dot_general | solution.py:50
  24.3 0.2 dynamic-update-slice
  24.5 8.4 %all-reduce = f32[8]{0:T(128)S(1)} all-reduce(f32[8]{0:T(128)S(1)} %dynamic-update-slice), channel_id=2, replica_groups=mesh['dp'=8,'section'=4] {'section'}, use_global_device_ids=true, to_apply=%add | all-reduce | flops 8 | bytes 64
  32.8 0.1 reshape.49
  32.9 0.1 while.16
  33.1 5.8 %psum.7 = f32[2]{0:T(128)S(1)} all-reduce(f32[2]{0:T(128)S(1)} %broadcast_select_fusion.2), channel_id=1, replica_groups=mesh['dp'=8,'section'=4] {'section'}, use_global_device_ids=true, to_apply=%region_3.4 | all-reduce | flops 2 | bytes 16 | tf_op jit(solution)/shard_map/psum | solution.py:25
  38.9 0.5 maximum_divide_fusion
  39.4 0.0 copy-done
  39.4 14.9 %fusion.3 = bf16[4096,1024]{0,1:T(8,128)(2,1)} fusion(bf16[1,2,512,4096]{3,2,1,0:T(8,128)(2,1)} %param.5, f32[2]{0:T(128)S(1)} %get-tuple-element.140, bf16[1,2,512,1024]{3,2,1,0:T(8,128)(2,1)S(1)} %copy-done, bf16[2,512]{1,0:T(2,128)(2,1)S(1)} %compare_convert_fusion), kind=kOutput, calls=%fused_computation.6 | convolution fusion | flops 8598323200 | bytes 18876424 | tf_op jit(solution)/shard_map/dot_general | solution.py:34
  54.3 0.0 reduce-scatter.2.cloned.1.call-update
  54.3 148.4 %reduce-scatter.2.cloned.1.call-done = bf16[512,1024]{0,1:T(8,128)(2,1)} async-done(((bf16[4096,1024]{0,1:T(8,128)(2,1)}), bf16[512,1024]{0,1:T(8,128)(2,1)}) %reduce-scatter.2.cloned.1.call-update) | async-done | bytes 1048592 | tf_op jit(solution)/shard_map/reduce_scatter | solution.py:64
  202.7 1.4 fusion.15
  204.1 1.3 copy.8
  (7 shorter events, 0.1 us)
Async XLA Ops:
  7.2 195.5 %reduce-scatter.2.cloned.1.call-start = ((), (), s32[]{:S(2)}) async-start(), calls=%async_computation.1 | async-start | bytes 9437184 | tf_op jit(solution)/shard_map/reduce_scatter | solution.py:64
  13.6 25.8 %copy-start = (bf16[1,2,512,1024]{3,2,1,0:T(8,128)(2,1)S(1)}, bf16[1,2,512,1024]{3,2,1,0:T(8,128)(2,1)}, u32[]{:S(2)}) copy-start(bf16[1,2,512,1024]{3,2,1,0:T(8,128)(2,1)} %param.6) | copy-start | bytes 6291460
Sparse Core Ops, SparseCore 0:
  54.4 148.2 reduce-scatter.1
where the time goes:
time: 213 us; the launch traced here: 212 us
  waiting for transfers between devices  148 us (69%)
  matrix products  29.1 us (14%)
  between operations  14.8 us (7%)
  blocking collectives  14.1 us (7%)
  local copies, waits for them, and re-layouts  2.91 us (1%)
  other arithmetic  2.74 us (1%)
    reduce_scatter x1, waiting for transfers between devices, on_device(): lax.psum_scatter(row_term(flat_acts, flat_scaled, 0).astype(jnp.bfloat16)...  148 us
    dot_general x1, matrix products, row_term(): lax.dot_general(columns, flat_scaled[layer_index], (((0,), (0,)), ((), ()...  14.9 us
    dot_general x1, matrix products, on_device(): jnp.einsum('lesd,letd->lest', activations, activations, preferred_element...  10.7 us
    unnamed x1, blocking collectives  8.38 us
    psum x1, blocking collectives, from_root(): return lax.psum(kept, axis)  5.76 us
  transfers between devices with their start and end apart: 1, of which 1 were waited for; matrix products, arithmetic and copies ran while one was open for 0% of the time, Pallas kernels for 0%

commit v1 on v0

v1 whole, which is shorter than its diff:
```python
import functools
import math

import jax
import jax.numpy as jnp
from jax import lax
from jax.experimental import pallas as pl
from jax.experimental.pallas import tpu as pltpu
from jax.sharding import PartitionSpec as P

MESH = pl.DeviceIdType.MESH
F32 = jnp.float32


def gram(rows, others):
    return lax.dot_general(rows, others, (((1,), (1,)), ((), ())), preferred_element_type=F32)


def kernel(
    plan,
    lengths_ref,
    acts_hbm,
    grads_hbm,
    out_ref,
    ratio_ref,
    acts,
    grads,
    norm_mine,
    norm_slots,
    pair_out,
    pair_in,
    line_out,
    line_in,
    load_sems,
    norm_send,
    norm_recv,
    pair_send,
    pair_recv,
    line_send,
    line_recv,
):
    examples, seq, outer, inner, sections, rows, subs, bound, examples_all = plan
    width = acts.shape[1]
    block = rows * subs
    place = lax.axis_index("dp")
    section = lax.axis_index("section")
    across = lax.rem(place, inner)
    along = lax.div(place, inner)
    partner = along * inner + (inner - 1 - across)

    loads = []
    for e in range(examples):
        span = pl.ds(e * seq, seq)
        copy = pltpu.make_async_copy(grads_hbm.at[span], grads.at[span], load_sems.at[e])
        copy.start()
        loads.append(copy)
    for e in range(examples):
        span = pl.ds(e * seq, seq)
        copy = pltpu.make_async_copy(
            acts_hbm.at[span], acts.at[span], load_sems.at[examples + e]
        )
        copy.start()
        loads.append(copy)

    barrier = pltpu.get_barrier_semaphore()
    for step in range(1, sections):
        peer = lax.rem(section + step, sections)
        pl.semaphore_signal(barrier, inc=1, device_id={"section": peer}, device_id_type=MESH)
    pl.semaphore_signal(barrier, inc=1, device_id={"dp": partner}, device_id_type=MESH)
    for step in range(1, outer):
        peer = lax.rem(along + step, outer) * inner + across
        pl.semaphore_signal(barrier, inc=1, device_id={"dp": peer}, device_id_type=MESH)

    half = seq // 2
    tile_row = lax.broadcasted_iota(jnp.int32, norm_mine.shape, 0)
    mine = jnp.zeros(norm_mine.shape, F32)
    for e in range(examples):
        base = e * seq
        span = pl.ds(base, seq)
        top, bottom = pl.ds(base, half), pl.ds(base + half, half)
        loads[e].wait()
        token = lax.broadcasted_iota(jnp.int32, (seq, grads.shape[1]), 0)
        keep = (token < lengths_ref[e]).astype(F32)
        grads[span] = (grads[span].astype(F32) * keep).astype(jnp.bfloat16)
        grad_top = gram(grads[top], grads[span])
        grad_low = gram(grads[bottom], grads[bottom])
        loads[examples + e].wait()
        prod_top = gram(acts[top], acts[span]) * grad_top
        prod_low = gram(acts[bottom], acts[bottom]) * grad_low
        norm = (
            jnp.sum(prod_top[:, :half])
            + 2.0 * jnp.sum(prod_top[:, half:])
            + jnp.sum(prod_low)
        )
        mine = jnp.where(tile_row == e, norm, mine)
    norm_mine[...] = mine
    norm_slots[section] = mine

    pl.semaphore_wait(barrier, sections - 1 + 1 + outer - 1)

    norm_copies = []
    for step in range(1, sections):
        peer = lax.rem(section + step, sections)
        copy = pltpu.make_async_remote_copy(
            src_ref=norm_mine,
            dst_ref=norm_slots.at[section],
            send_sem=norm_send.at[step],
            recv_sem=norm_recv.at[step],
            device_id={"section": peer},
            device_id_type=MESH,
        )
        copy.start()
        norm_copies.append(copy)
    for copy in norm_copies:
        copy.wait()
    total = norm_slots[0]
    for s in range(1, sections):
        total = total + norm_slots[s]
    ratio = jnp.sqrt(total) / bound
    ratio_ref[...] = ratio
    factor = 1.0 / jnp.maximum(ratio, 1.0)
    for e in range(examples):
        span = pl.ds(e * seq, seq)
        scale = factor[e : e + 1, 0:1]
        grads[span] = (grads[span].astype(F32) * scale).astype(jnp.bfloat16)

    def partial(line, side, sub):
        start = (line * inner + side) * block + sub * rows
        columns = pl.ds(pl.multiple_of(start, rows), rows)
        return lax.dot_general(
            acts[:, columns], grads[...], (((0,), (0,)), ((), ())), preferred_element_type=F32
        )

    def target(k):
        return lax.rem(along + 1 + lax.div(k, subs), outer), lax.rem(k, subs)

    def pair_copy(k):
        return pltpu.make_async_remote_copy(
            src_ref=pair_out.at[k],
            dst_ref=pair_in.at[k],
            send_sem=pair_send.at[k],
            recv_sem=pair_recv.at[k],
            device_id={"dp": partner},
            device_id_type=MESH,
        )

    def line_copy(k):
        line, sub = target(k)
        return pltpu.make_async_remote_copy(
            src_ref=line_out.at[k],
            dst_ref=line_in.at[k],
            send_sem=line_send.at[k],
            recv_sem=line_recv.at[k],
            device_id={"dp": line * inner + across},
            device_id_type=MESH,
        )

    chunks = outer * subs
    remote = (outer - 1) * subs

    @pl.loop(0, chunks)
    def _(k):
        line, sub = target(k)
        pair_out[k] = partial(line, inner - 1 - across, sub).astype(jnp.bfloat16)
        pair_copy(k).start()

    @pl.loop(0, remote)
    def _(k):
        line, sub = target(k)
        own = partial(line, across, sub)
        pair_copy(k).wait_recv()
        line_out[k] = (own + pair_in[k].astype(F32)).astype(jnp.bfloat16)
        line_copy(k).start()

    @pl.loop(0, subs)
    def _(sub):
        own = partial(along, across, sub)
        pair_copy(remote + sub).wait_recv()
        own = own + pair_in[remote + sub].astype(F32)
        for step in range(outer - 1):
            line_copy(step * subs + sub).wait_recv()
            own = own + line_in[step * subs + sub].astype(F32)
        into = pl.ds(pl.multiple_of(sub * rows, rows), rows)
        out_ref[into] = (own / examples_all).astype(jnp.bfloat16)

    @pl.loop(0, chunks)
    def _(k):
        pair_copy(k).wait_send()

    @pl.loop(0, remote)
    def _(k):
        line_copy(k).wait_send()


def on_device(sections, places, activations, out_grads, lengths):
    layers, examples, seq, width = activations.shape
    features = out_grads.shape[3]
    inner = 2
    outer = places // inner
    block = width // places
    rows = min(block, 128)
    subs = block // rows
    bound = 0.5 * math.sqrt(float(layers * sections * seq * width * features))
    plan = (examples, seq, outer, inner, sections, rows, subs, bound, float(places * examples))
    chunks = outer * subs
    remote = (outer - 1) * subs
    tokens = examples * seq
    tile = (max(8, -(-examples // 8) * 8), 128)
    dma = pltpu.SemaphoreType.DMA
    bf16 = jnp.bfloat16
    grad, ratio = pl.pallas_call(
        functools.partial(kernel, plan),
        out_shape=(
            jax.ShapeDtypeStruct((block, features), bf16),
            jax.ShapeDtypeStruct(tile, F32),
        ),
        in_specs=[
            pl.BlockSpec(memory_space=pltpu.SMEM),
            pl.BlockSpec(memory_space=pl.ANY),
            pl.BlockSpec(memory_space=pl.ANY),
        ],
        out_specs=(
            pl.BlockSpec(memory_space=pltpu.VMEM),
            pl.BlockSpec(memory_space=pltpu.VMEM),
        ),
        scratch_shapes=[
            pltpu.VMEM((tokens, width), bf16),
            pltpu.VMEM((tokens, features), bf16),
            pltpu.VMEM(tile, F32),
            pltpu.VMEM((sections,) + tile, F32),
            pltpu.VMEM((chunks, rows, features), bf16),
            pltpu.VMEM((chunks, rows, features), bf16),
            pltpu.VMEM((remote, rows, features), bf16),
            pltpu.VMEM((remote, rows, features), bf16),
            dma((2 * examples,)),
            dma((sections,)),
            dma((sections,)),
            dma((chunks,)),
            dma((chunks,)),
            dma((remote,)),
            dma((remote,)),
        ],
        compiler_params=pltpu.CompilerParams(
            collective_id=0, has_side_effects=True, vmem_limit_bytes=56 * 2**20
        ),
    )(
        lengths,
        activations.reshape(tokens, width),
        out_grads.reshape(tokens, features),
    )
    return grad[None], ratio[:examples, 0]


def solution(mesh):
    placed = (P("section", "dp", None, None), P("section", "dp", None, None), P("dp"))
    return jax.shard_map(
        functools.partial(on_device, mesh.shape["section"], mesh.shape["dp"]),
        mesh=mesh,
        in_specs=placed,
        out_specs=(P("section", "dp", None), P("dp")),
        check_vma=False,
    )
```

time: 213 us -> 122 us (0.57)
  waiting for transfers between devices: 148 us -> 0 us
  Pallas kernels: 0 us -> 117 us
  matrix products: 29.1 us -> 0 us
  between operations: 14.8 us -> 0.64 us
  blocking collectives: 14.1 us -> 0 us
  other arithmetic: 2.74 us -> 0 us
    reduce_scatter x1 -> x0, waiting for transfers between devices: 148 us -> none  [on_device(): lax.psum_scatter(row_term(flat_acts, flat_scaled, 0).astype(jnp.bfloat16)...]
    pallas_call x0 -> x1, Pallas kernels: none -> 117 us  [on_device(): pl.pallas_call(functools.partial(kernel, plan), out_shape=(jax.ShapeDtype...]
    dot_general x3 -> x0, matrix products: 29.1 us -> none  [the longest x1 14.9 us: row_term(): lax.dot_general(columns, flat_scaled[layer_index], (((0,), (0,)), ((), ()...]
    unnamed x1 -> x0, blocking collectives: 8.38 us -> none
    psum x1 -> x0, blocking collectives: 5.76 us -> none  [from_root(): return lax.psum(kept, axis)]
    convert_element_type x2 -> x0, other arithmetic: 2.14 us -> none  [the longest x1 1.41 us: on_device(): mean_grad = (stacked / examples_all).astype(jnp.bfloat16)]
  transfers between devices with their start and end apart: 1 -> 0, of which waited for: 1 -> 0; matrix products, arithmetic and copies ran while one was open for 0% -> 0% of each run, Pallas kernels for 0% -> 0%
where the time goes in v1:
time: 122 us
  Pallas kernels  117 us (96%)
  local copies, waits for them, and re-layouts  3.56 us (3%)
    pallas_call x1, Pallas kernels, on_device(): pl.pallas_call(functools.partial(kernel, plan), out_shape=(jax.ShapeDtype...  117 us

profile of v1, /device:TPU:0, one launch (start us, length us, event | category | flops | bytes accessed | tf_op | source)
XLA Modules:
  0.0 121.6 jit_solution(16635278013840182111)
XLA Ops:
  0.6 117.4 %shard_map.50 = (bf16[512,1024]{1,0:T(8,128)(2,1)}, f32[8,128]{1,0:T(8,128)}) custom-call(s32[2]{0:T(128)} %lengths_ref.1, bf16[1024,4096]{1,0:T(8,128)(2,1)} %bitcast.3, bf16[1024,1024]{1,0:T(8,128)(2,1)} %bitcast.4), custom_call_target="tpu_custom_call" | custom-call | tf_op jit(solution)/shard_map/pallas_call | solution.py:211
  118.1 1.3 %slice_reduce_fusion = f32[2]{0:T(128)} fusion(f32[8,128]{1,0:T(8,128)} %get-tuple-element.5), kind=kLoop, calls=%fused_computation | loop fusion | bytes 16 | tf_op jit(solution)/shard_map/slice | solution.py:251
  119.4 2.3 %copy.6 = bf16[1,512,1024]{2,1,0:T(8,128)(2,1)} copy(bf16[1,512,1024]{2,1,0:T(8,128)(2,1)} %bitcast.5) | data formatting | bytes 2097152

commit v2 on v1

--- a/solution.py
+++ b/solution.py
@@ -117,7 +117,10 @@
     for s in range(1, sections):
         total = total + norm_slots[s]
     ratio = jnp.sqrt(total) / bound
-    ratio_ref[...] = ratio
+    first_column = lax.broadcasted_iota(jnp.int32, norm_mine.shape, 1) == 0
+    for e in range(examples):
+        chosen = jnp.logical_and(tile_row == e, first_column)
+        ratio_ref[e] = jnp.sum(jnp.where(chosen, ratio, 0.0))
     factor = 1.0 / jnp.maximum(ratio, 1.0)
     for e in range(examples):
         span = pl.ds(e * seq, seq)
@@ -131,8 +134,17 @@
             acts[:, columns], grads[...], (((0,), (0,)), ((), ())), preferred_element_type=F32
         )
 
+    relayed = outer == 4
+    far_half = lax.div(along, 2)
+    at_end = jnp.logical_or(along == 0, along == outer - 1)
+
     def target(k):
-        return lax.rem(along + 1 + lax.div(k, subs), outer), lax.rem(k, subs)
+        turn, sub = lax.div(k, subs), lax.rem(k, subs)
+        if not relayed:
+            return lax.rem(along + 1 + turn, outer), sub
+        mirrored = jnp.where(far_half == 1, outer - 1 - along, along)
+        line = lax.rem(outer - 1 + mirrored - turn + outer, outer)
+        return jnp.where(far_half == 1, outer - 1 - line, line), sub
 
     def pair_copy(k):
         return pltpu.make_async_remote_copy(
@@ -144,16 +156,28 @@
             device_id_type=MESH,
         )
 
+    def landing(k, slot, line):
+        return pltpu.make_async_remote_copy(
+            src_ref=line_out.at[k],
+            dst_ref=line_in.at[slot],
+            send_sem=line_send.at[k],
+            recv_sem=line_recv.at[slot],
+            device_id={"dp": line * inner + across},
+            device_id_type=MESH,
+        )
+
+    def crosses(line):
+        return lax.div(line, 2) != far_half
+
     def line_copy(k):
         line, sub = target(k)
-        return pltpu.make_async_remote_copy(
-            src_ref=line_out.at[k],
-            dst_ref=line_in.at[k],
-            send_sem=line_send.at[k],
-            recv_sem=line_recv.at[k],
-            device_id={"dp": line * inner + across},
-            device_id_type=MESH,
-        )
+        if not relayed:
+            return landing(k, k, line)
+        handed = jnp.logical_and(at_end, crosses(line))
+        direct = jnp.where(crosses(line), 1, 0)
+        slot = jnp.where(handed, 2 + lax.rem(line, 2), direct)
+        stop = jnp.where(at_end, jnp.where(along == 0, 1, outer - 2), line)
+        return landing(k, slot * subs + sub, stop)
 
     chunks = outer * subs
     remote = (outer - 1) * subs
@@ -169,7 +193,22 @@
         line, sub = target(k)
         own = partial(line, across, sub)
         pair_copy(k).wait_recv()
-        line_out[k] = (own + pair_in[k].astype(F32)).astype(jnp.bfloat16)
+        own = own + pair_in[k].astype(F32)
+        if relayed:
+            adds = jnp.logical_and(jnp.logical_not(at_end), crosses(line))
+
+            @pl.when(adds)
+            def _():
+                slot = (2 + lax.rem(line, 2)) * subs + sub
+                landing(k, slot, line).wait_recv()
+                line_out[k] = (own + line_in[slot].astype(F32)).astype(jnp.bfloat16)
+
+            @pl.when(jnp.logical_not(adds))
+            def _():
+                line_out[k] = own.astype(jnp.bfloat16)
+
+        else:
+            line_out[k] = own.astype(jnp.bfloat16)
         line_copy(k).start()
 
     @pl.loop(0, subs)
@@ -177,9 +216,10 @@
         own = partial(along, across, sub)
         pair_copy(remote + sub).wait_recv()
         own = own + pair_in[remote + sub].astype(F32)
-        for step in range(outer - 1):
-            line_copy(step * subs + sub).wait_recv()
-            own = own + line_in[step * subs + sub].astype(F32)
+        for step in range(2 if relayed else outer - 1):
+            slot = step * subs + sub
+            landing(slot, slot, along).wait_recv()
+            own = own + line_in[slot].astype(F32)
         into = pl.ds(pl.multiple_of(sub * rows, rows), rows)
         out_ref[into] = (own / examples_all).astype(jnp.bfloat16)
 
@@ -212,7 +252,7 @@
         functools.partial(kernel, plan),
         out_shape=(
             jax.ShapeDtypeStruct((block, features), bf16),
-            jax.ShapeDtypeStruct(tile, F32),
+            jax.ShapeDtypeStruct((examples,), F32),
         ),
         in_specs=[
             pl.BlockSpec(memory_space=pltpu.SMEM),
@@ -221,7 +261,7 @@
         ],
         out_specs=(
             pl.BlockSpec(memory_space=pltpu.VMEM),
-            pl.BlockSpec(memory_space=pltpu.VMEM),
+            pl.BlockSpec(memory_space=pltpu.SMEM),
         ),
         scratch_shapes=[
             pltpu.VMEM((tokens, width), bf16),
@@ -231,14 +271,14 @@
             pltpu.VMEM((chunks, rows, features), bf16),
             pltpu.VMEM((chunks, rows, features), bf16),
             pltpu.VMEM((remote, rows, features), bf16),
-            pltpu.VMEM((remote, rows, features), bf16),
+            pltpu.VMEM((chunks, rows, features), bf16),
             dma((2 * examples,)),
             dma((sections,)),
             dma((sections,)),
             dma((chunks,)),
             dma((chunks,)),
             dma((remote,)),
-            dma((remote,)),
+            dma((chunks,)),
         ],
         compiler_params=pltpu.CompilerParams(
             collective_id=0, has_side_effects=True, vmem_limit_bytes=56 * 2**20
@@ -248,7 +288,7 @@
         activations.reshape(tokens, width),
         out_grads.reshape(tokens, features),
     )
-    return grad[None], ratio[:examples, 0]
+    return grad[None], ratio
 
 
 def solution(mesh):

time: 122 us -> 114 us (0.934)
  Pallas kernels: 117 us -> 110 us
    pallas_call x1, Pallas kernels: 117 us -> 110 us  [on_device(): pl.pallas_call(functools.partial(kernel, plan), out_shape=(jax.ShapeDtype...]
    slice x1 -> x0, local copies, waits for them, and re-layouts: 1.3 us -> none  [on_device(): return (grad[None], ratio[:examples, 0])]
    unnamed x1 -> x2, local copies, waits for them, and re-layouts: 2.26 us -> 3.38 us
where the time goes in v2:
time: 114 us
  Pallas kernels  110 us (96%)
  local copies, waits for them, and re-layouts  3.38 us (3%)
    pallas_call x1, Pallas kernels, on_device(): pl.pallas_call(functools.partial(kernel, plan), out_shape=(jax.ShapeDtype...  110 us
    unnamed x2, local copies, waits for them, and re-layouts  3.38 us

profile of v2, /device:TPU:0, one launch (start us, length us, event | category | flops | bytes accessed | tf_op | source)
XLA Modules:
  0.0 114.1 jit_solution(15382999083706812563)
XLA Ops:
  0.6 110.1 %shard_map.50 = (bf16[512,1024]{1,0:T(8,128)(2,1)}, f32[2]{0:T(128)}) custom-call(s32[2]{0:T(128)} %lengths_ref.1, bf16[1024,4096]{1,0:T(8,128)(2,1)} %bitcast.3, bf16[1024,1024]{1,0:T(8,128)(2,1)} %bitcast.4), custom_call_target="tpu_custom_call" | custom-call | tf_op jit(solution)/shard_map/pallas_call | solution.py:251
  110.7 2.3 %copy.7 = bf16[1,512,1024]{2,1,0:T(8,128)(2,1)} copy(bf16[1,512,1024]{2,1,0:T(8,128)(2,1)} %bitcast.5) | data formatting | bytes 2097152
  113.0 1.1 copy.8

commit v3 on v2

--- a/solution.py
+++ b/solution.py
@@ -31,6 +31,9 @@
     pair_in,
     line_out,
     line_in,
+    late_out,
+    late_in,
+    total_ref,
     load_sems,
     norm_send,
     norm_recv,
@@ -38,6 +41,8 @@
     pair_recv,
     line_send,
     line_recv,
+    late_send,
+    late_recv,
 ):
     examples, seq, outer, inner, sections, rows, subs, bound, examples_all = plan
     width = acts.shape[1]
@@ -156,60 +161,120 @@
             device_id_type=MESH,
         )
 
-    def landing(k, slot, line):
+    def copy_along(bufs, k, slot, line):
+        source, land, send, recv = bufs
         return pltpu.make_async_remote_copy(
-            src_ref=line_out.at[k],
-            dst_ref=line_in.at[slot],
-            send_sem=line_send.at[k],
-            recv_sem=line_recv.at[slot],
+            src_ref=source.at[k],
+            dst_ref=land.at[slot],
+            send_sem=send.at[k],
+            recv_sem=recv.at[slot],
             device_id={"dp": line * inner + across},
             device_id_type=MESH,
         )
 
+    landing = functools.partial(copy_along, (line_out, line_in, line_send, line_recv))
+    late_landing = functools.partial(copy_along, (late_out, late_in, late_send, late_recv))
+
     def crosses(line):
         return lax.div(line, 2) != far_half
+
+    def adds(line):
+        return jnp.logical_and(jnp.logical_not(at_end), crosses(line))
+
+    def route(line):
+        handed = jnp.logical_and(at_end, crosses(line))
+        direct = jnp.where(crosses(line), 1, 0)
+        slot = jnp.where(handed, 2 + lax.rem(line, 2), direct)
+        stop = jnp.where(at_end, jnp.where(along == 0, 1, outer - 2), line)
+        return slot, stop
 
     def line_copy(k):
         line, sub = target(k)
         if not relayed:
             return landing(k, k, line)
-        handed = jnp.logical_and(at_end, crosses(line))
-        direct = jnp.where(crosses(line), 1, 0)
-        slot = jnp.where(handed, 2 + lax.rem(line, 2), direct)
-        stop = jnp.where(at_end, jnp.where(along == 0, 1, outer - 2), line)
+        slot, stop = route(line)
         return landing(k, slot * subs + sub, stop)
+
+    def late_copy(turn, line):
+        slot, stop = route(line)
+        return late_landing(turn, slot, stop)
+
+    def late_line(line):
+        return line != 2
+
+    def is_late(line, sub):
+        if not relayed:
+            return jnp.bool_(False)
+        return jnp.logical_and(sub == subs - 1, late_line(line))
 
     chunks = outer * subs
     remote = (outer - 1) * subs
 
-    @pl.loop(0, chunks)
-    def _(k):
+    def exchange(k):
         line, sub = target(k)
-        pair_out[k] = partial(line, inner - 1 - across, sub).astype(jnp.bfloat16)
-        pair_copy(k).start()
-
-    @pl.loop(0, remote)
-    def _(k):
+
+        @pl.when(jnp.logical_not(is_late(line, sub)))
+        def _():
+            pair_out[k] = partial(line, inner - 1 - across, sub).astype(jnp.bfloat16)
+            pair_copy(k).start()
+
+    def late(turn):
+        line, _ = target(turn * subs)
+
+        @pl.when(late_line(line))
+        def _():
+            total_ref[...] = partial(line, inner - 1 - across, subs - 1)
+
+            @pl.when(adds(line))
+            def _():
+                slot = 2 + lax.rem(line, 2)
+                late_landing(turn, slot, line).wait_recv()
+                total_ref[...] += late_in[slot].astype(F32)
+
+            late_out[turn] = total_ref[...].astype(jnp.bfloat16)
+            late_copy(turn, line).start()
+
+    pl.loop(0, 1)(exchange)
+    if relayed:
+        pl.loop(0, 1)(late)
+    pl.loop(1, chunks)(exchange)
+    if relayed:
+        pl.loop(1, outer - 1)(late)
+
+    def forward(k):
         line, sub = target(k)
-        own = partial(line, across, sub)
-        pair_copy(k).wait_recv()
-        own = own + pair_in[k].astype(F32)
+        total_ref[...] = partial(line, across, sub)
+
+        @pl.when(jnp.logical_not(is_late(line, sub)))
+        def _():
+            pair_copy(k).wait_recv()
+            total_ref[...] += pair_in[k].astype(F32)
+
         if relayed:
-            adds = jnp.logical_and(jnp.logical_not(at_end), crosses(line))
-
-            @pl.when(adds)
+
+            @pl.when(adds(line))
             def _():
                 slot = (2 + lax.rem(line, 2)) * subs + sub
                 landing(k, slot, line).wait_recv()
-                line_out[k] = (own + line_in[slot].astype(F32)).astype(jnp.bfloat16)
-
-            @pl.when(jnp.logical_not(adds))
-            def _():
-                line_out[k] = own.astype(jnp.bfloat16)
-
-        else:
-            line_out[k] = own.astype(jnp.bfloat16)
+                total_ref[...] += line_in[slot].astype(F32)
+
+        line_out[k] = total_ref[...].astype(jnp.bfloat16)
         line_copy(k).start()
+
+    pl.loop(0, subs)(forward)
+
+    if relayed:
+
+        @pl.when(late_line(along))
+        def _():
+            own = partial(along, inner - 1 - across, subs - 1)
+            for slot in range(2):
+                late_landing(slot, slot, along).wait_recv()
+                own = own + late_in[slot].astype(F32)
+            pair_out[chunks - 1] = own.astype(jnp.bfloat16)
+            pair_copy(chunks - 1).start()
+
+    pl.loop(subs, remote)(forward)
 
     @pl.loop(0, subs)
     def _(sub):
@@ -225,7 +290,21 @@
 
     @pl.loop(0, chunks)
     def _(k):
-        pair_copy(k).wait_send()
+        line, sub = target(k)
+
+        @pl.when(jnp.logical_not(jnp.logical_and(is_late(line, sub), k < remote)))
+        def _():
+            pair_copy(k).wait_send()
+
+    if relayed:
+
+        @pl.loop(0, outer - 1)
+        def _(turn):
+            line, _ = target(turn * subs)
+
+            @pl.when(late_line(line))
+            def _():
+                late_copy(turn, line).wait_send()
 
     @pl.loop(0, remote)
     def _(k):
@@ -272,6 +351,9 @@
             pltpu.VMEM((chunks, rows, features), bf16),
             pltpu.VMEM((remote, rows, features), bf16),
             pltpu.VMEM((chunks, rows, features), bf16),
+            pltpu.VMEM((outer - 1, rows, features), bf16),
+            pltpu.VMEM((4, rows, features), bf16),
+            pltpu.VMEM((rows, features), F32),
             dma((2 * examples,)),
             dma((sections,)),
             dma((sections,)),
@@ -279,6 +361,8 @@
             dma((chunks,)),
             dma((remote,)),
             dma((chunks,)),
+            dma((outer - 1,)),
+            dma((4,)),
         ],
         compiler_params=pltpu.CompilerParams(
             collective_id=0, has_side_effects=True, vmem_limit_bytes=56 * 2**20

time: 114 us -> 103 us (0.904)
  Pallas kernels: 110 us -> 98.8 us
    pallas_call x1, Pallas kernels: 110 us -> 98.8 us  [on_device(): pl.pallas_call(functools.partial(kernel, plan), out_shape=(jax.ShapeDtype...]
where the time goes in v3:
time: 103 us
  Pallas kernels  98.8 us (96%)
  local copies, waits for them, and re-layouts  3.38 us (3%)
    pallas_call x1, Pallas kernels, on_device(): pl.pallas_call(functools.partial(kernel, plan), out_shape=(jax.ShapeDtype...  98.8 us
    unnamed x2, local copies, waits for them, and re-layouts  3.38 us

profile of v3, /device:TPU:0, one launch (start us, length us, event | category | flops | bytes accessed | tf_op | source)
XLA Modules:
  0.0 102.8 jit_solution(4190521336425008929)
XLA Ops:
  0.6 98.8 %shard_map.50 = (bf16[512,1024]{1,0:T(8,128)(2,1)}, f32[2]{0:T(128)}) custom-call(s32[2]{0:T(128)} %lengths_ref.1, bf16[1024,4096]{1,0:T(8,128)(2,1)} %bitcast.3, bf16[1024,1024]{1,0:T(8,128)(2,1)} %bitcast.4), custom_call_target="tpu_custom_call" | custom-call | tf_op jit(solution)/shard_map/pallas_call | solution.py:330
  99.4 2.3 %copy.7 = bf16[1,512,1024]{2,1,0:T(8,128)(2,1)} copy(bf16[1,512,1024]{2,1,0:T(8,128)(2,1)} %bitcast.5) | data formatting | bytes 2097152
  101.7 1.1 %copy.8 = f32[2]{0:T(128)} copy(f32[2]{0:T(128)} %get-tuple-element.9) | data formatting | bytes 16

commit v4 on v3

--- a/solution.py
+++ b/solution.py
@@ -58,14 +58,11 @@
         span = pl.ds(e * seq, seq)
         copy = pltpu.make_async_copy(grads_hbm.at[span], grads.at[span], load_sems.at[e])
         copy.start()
-        loads.append(copy)
-    for e in range(examples):
-        span = pl.ds(e * seq, seq)
-        copy = pltpu.make_async_copy(
+        more = pltpu.make_async_copy(
             acts_hbm.at[span], acts.at[span], load_sems.at[examples + e]
         )
-        copy.start()
-        loads.append(copy)
+        more.start()
+        loads.append((copy, more))
 
     barrier = pltpu.get_barrier_semaphore()
     for step in range(1, sections):
@@ -83,20 +80,25 @@
         base = e * seq
         span = pl.ds(base, seq)
         top, bottom = pl.ds(base, half), pl.ds(base + half, half)
-        loads[e].wait()
-        token = lax.broadcasted_iota(jnp.int32, (seq, grads.shape[1]), 0)
-        keep = (token < lengths_ref[e]).astype(F32)
-        grads[span] = (grads[span].astype(F32) * keep).astype(jnp.bfloat16)
+        grads_load, acts_load = loads[e]
+        grads_load.wait()
         grad_top = gram(grads[top], grads[span])
         grad_low = gram(grads[bottom], grads[bottom])
-        loads[examples + e].wait()
+        acts_load.wait()
         prod_top = gram(acts[top], acts[span]) * grad_top
         prod_low = gram(acts[bottom], acts[bottom]) * grad_low
-        norm = (
-            jnp.sum(prod_top[:, :half])
-            + 2.0 * jnp.sum(prod_top[:, half:])
-            + jnp.sum(prod_low)
-        )
+        length = lengths_ref[e]
+        at_row = lax.broadcasted_iota(jnp.int32, (half, half), 0)
+        at_col = lax.broadcasted_iota(jnp.int32, (half, half), 1)
+        latest = jnp.maximum(at_row, at_col)
+        entries = jnp.where(latest < length, prod_top[:, :half], 0.0)
+        entries += jnp.where(
+            jnp.logical_and(at_row < length, at_col + half < length),
+            2.0 * prod_top[:, half:],
+            0.0,
+        )
+        entries += jnp.where(latest + half < length, prod_low, 0.0)
+        norm = jnp.sum(entries, keepdims=True)
         mine = jnp.where(tile_row == e, norm, mine)
     norm_mine[...] = mine
     norm_slots[section] = mine
@@ -122,14 +124,11 @@
     for s in range(1, sections):
         total = total + norm_slots[s]
     ratio = jnp.sqrt(total) / bound
-    first_column = lax.broadcasted_iota(jnp.int32, norm_mine.shape, 1) == 0
-    for e in range(examples):
-        chosen = jnp.logical_and(tile_row == e, first_column)
-        ratio_ref[e] = jnp.sum(jnp.where(chosen, ratio, 0.0))
     factor = 1.0 / jnp.maximum(ratio, 1.0)
     for e in range(examples):
         span = pl.ds(e * seq, seq)
-        scale = factor[e : e + 1, 0:1]
+        token = lax.broadcasted_iota(jnp.int32, (seq, 1), 0)
+        scale = jnp.where(token < lengths_ref[e], factor[e : e + 1, 0:1], 0.0)
         grads[span] = (grads[span].astype(F32) * scale).astype(jnp.bfloat16)
 
     def partial(line, side, sub):
@@ -240,6 +239,11 @@
     pl.loop(1, chunks)(exchange)
     if relayed:
         pl.loop(1, outer - 1)(late)
+
+    first_column = lax.broadcasted_iota(jnp.int32, norm_mine.shape, 1) == 0
+    for e in range(examples):
+        chosen = jnp.logical_and(tile_row == e, first_column)
+        ratio_ref[e] = jnp.sum(jnp.where(chosen, ratio, 0.0))
 
     def forward(k):
         line, sub = target(k)

time: 103 us -> 103 us (level)
  no operation moved by 1% of the time
where the time goes in v4:
time: 103 us
  Pallas kernels  98.6 us (96%)
  local copies, waits for them, and re-layouts  3.38 us (3%)
    pallas_call x1, Pallas kernels, on_device(): pl.pallas_call(functools.partial(kernel, plan), out_shape=(jax.ShapeDtype...  98.6 us
    unnamed x2, local copies, waits for them, and re-layouts  3.38 us

profile of v4, /device:TPU:0, one launch (start us, length us, event | category | flops | bytes accessed | tf_op | source)
XLA Modules:
  0.0 102.6 jit_solution(7947811805240502343)
XLA Ops:
  0.6 98.6 %shard_map.50 = (bf16[512,1024]{1,0:T(8,128)(2,1)}, f32[2]{0:T(128)}) custom-call(s32[2]{0:T(128)} %lengths_ref.1, bf16[1024,4096]{1,0:T(8,128)(2,1)} %bitcast.3, bf16[1024,1024]{1,0:T(8,128)(2,1)} %bitcast.4), custom_call_target="tpu_custom_call" | custom-call | tf_op jit(solution)/shard_map/pallas_call | solution.py:334
  99.3 2.3 %copy.7 = bf16[1,512,1024]{2,1,0:T(8,128)(2,1)} copy(bf16[1,512,1024]{2,1,0:T(8,128)(2,1)} %bitcast.5) | data formatting | bytes 2097152
  101.5 1.1 %copy.8 = f32[2]{0:T(128)} copy(f32[2]{0:T(128)} %get-tuple-element.9) | data formatting | bytes 16
